TPU v7x, 128 devices: a whole 4x4x4 slice. The times are simulated.
128 devices in a mesh: layer: 4 (over z_hi, core), dp: 32 (over y, z_lo, x).
Axes of the slice: x: 4, y: 4, z: 4 (z_hi: 2, z_lo: 2; z = z_hi * 2 + z_lo), core: 2. Of those that a mesh axis runs over, the one named last changes fastest.
Arguments:
- out_grads: bfloat16 [4, 128, 16384], P('layer', None, 'dp'), may hold values from -3 to 3
- in_acts: bfloat16 [4, 128, 4096], P('layer', None, 'dp'), may hold values from -3 to 3
- out_basis: bfloat16 [4, 16384, 16384], P('layer', None, 'dp'), may hold values from -0.046875 to 0.046875
- in_basis: bfloat16 [4, 4096, 4096], P('layer', None, 'dp'), may hold values from -0.09375 to 0.09375
- eigenvalues: bfloat16 [4, 16384, 4096], P('layer', 'dp'), may hold values from 0.5 to 50
- out_store: bfloat16 [4, 64, 32, 16384], P('layer', 'dp'), may hold values from -0.046875 to 0.046875
- in_store: bfloat16 [4, 64, 32, 4096], P('layer', 'dp'), may hold values from -0.09375 to 0.09375
- counts: int32 [64], P('dp'), may hold values from 1 to 4096
- winners: int32 [4, 6], replicated, may hold values from 0 to 63
Outputs:
- influence: float32 [4, 6, 32], replicated
All inputs are finite; a program needn't handle non-finite values.
Results may differ from a plain program's by a relative error of at most 0.0055.
Values may be sent and summed in bfloat16 or wider, within the bound.
No kernel may reach another device: no remote copies, remote signals or barrier semaphores. Data moves between devices by JAX's collectives and lax.ppermute only.
A program may use at most 192 MiB of HBM per device.

v0:
```python
import functools
import jax
import jax.numpy as jnp
from jax import lax
from jax.sharding import Mesh
from jax.sharding import PartitionSpec as P

NQ = 4
TQ = 32
WIN = 6
R = 32
SPAN = 128
DP = ("dp_0", "dp_1", "dp_2")
LAYER_DP = ("layer_0", "layer_1", "dp_0", "dp_1", "dp_2")
LAYER = ("layer_0", "layer_1")
damping = 0.1


def in_order(blocks, dim):
    blocks = jnp.moveaxis(blocks, 0, dim)
    shape = blocks.shape
    return blocks.reshape(*shape[:dim], shape[dim] * shape[dim + 1], *shape[dim + 2 :])


def all_blocks(value, axes, turns):
    blocks = value[None]
    for k in turns:
        blocks = lax.all_gather(blocks, axes[k], axis=0, tiled=True)
    block = [lax.axis_size(axes[k]) for k in reversed(turns)]
    blocks = blocks.reshape(*block, *value.shape)
    turned = sorted(range(len(turns)), key=lambda place: turns[len(turns) - 1 - place])
    return blocks.transpose(*turned, *range(len(turns), blocks.ndim)).reshape(-1, *value.shape)


def whole_of(value, axes, turns, dim):
    return in_order(all_blocks(value, axes, turns), dim)


def from_everyone(value, axis):
    count = lax.axis_size(axis)
    return lax.all_to_all(
        jnp.broadcast_to(value[None], (count, *value.shape)), axis, 0, 0, tiled=True
    )


def collect(value, axis, dim):
    return in_order(from_everyone(value, axis), dim)


def over_axes(value, axes):
    return functools.reduce(lax.psum, axes, value)


def on_device(
    out_grads, in_acts, out_basis, in_basis, eigenvalues, out_store, in_store, counts, winners
):
    out_local = out_basis[0]
    in_local = in_basis[0]
    out_width = out_local.shape[1]
    rows = out_local
    turned_out = jnp.dot(
        whole_of(out_grads[0], DP, (1, 0, 2), 1), rows, preferred_element_type=jnp.float32
    ).astype(jnp.bfloat16)
    rows = in_local
    turned_part = jnp.dot(
        collect(in_acts[0], DP, 1), rows, preferred_element_type=jnp.float32
    ).astype(jnp.bfloat16)
    turned_in = collect(turned_part, DP, 1)
    left = turned_out.reshape(NQ, TQ, out_width)
    right = turned_in.reshape(NQ, TQ, turned_in.shape[1])
    product = jnp.einsum("qtf,qtd->qfd", left, right, preferred_element_type=jnp.float32)
    divisor = eigenvalues[0].astype(jnp.float32) + damping
    precond = (product / divisor[None]).astype(jnp.bfloat16)
    alive = (jnp.arange(R, dtype=jnp.int32)[None, :] * SPAN < counts[:, None]).astype(jnp.bfloat16)
    masked = in_store[0] * alive[:, :, None]
    out_slices = lax.all_to_all(out_store[0], DP, split_axis=2, concat_axis=0, tiled=True)
    chosen = winners.reshape(NQ * WIN)
    left_rows = jnp.take(out_slices, chosen, axis=0).reshape(NQ, WIN * R, out_width)
    full_width = turned_in.shape[1]
    in_whole = lax.all_gather(masked, DP, axis=0, tiled=True)
    right_rows = jnp.take(in_whole, chosen, axis=0).reshape(NQ, WIN * R, full_width)
    mapped = jnp.einsum("qfd,qkd->qkf", precond, right_rows, preferred_element_type=jnp.float32)
    partial_value = jnp.sum(mapped * left_rows.astype(jnp.float32), axis=2)
    totals = over_axes(partial_value, LAYER_DP)
    return totals.reshape(NQ, WIN, R)


def solution(mesh):
    torus = Mesh(
        mesh.devices.reshape(2, 2, 4, 2, 4), ("layer_0", "layer_1", "dp_0", "dp_1", "dp_2")
    )
    return jax.shard_map(
        on_device,
        mesh=torus,
        in_specs=(
            P(LAYER, None, DP),
            P(LAYER, None, DP),
            P(LAYER, None, DP),
            P(LAYER, None, DP),
            P(LAYER, DP, None),
            P(LAYER, DP, None, None),
            P(LAYER, DP, None, None),
            P(DP),
            P(),
        ),
        out_specs=P(),
        check_vma=False,
    )
```

profile of v0, /device:TPU:8, one launch (start us, length us, event | category | flops | bytes accessed | tf_op | source)
XLA Modules:
  0.0 420.1 jit_solution(17354535812470855363)
XLA Ops:
  6.5 8.0 %all_gather.13 = bf16[2,128,512]{2,1,0:T(8,128)(2,1)} all-gather(bf16[1,128,512]{2,1,0:T(8,128)(2,1)} %param.9), channel_id=1, replica_groups=mesh['layer_0'=2,'layer_1'=2,'dp_0'=4,'dp_1'=2,'dp_2'=4] {'dp_1'}, dimensions={0}, use_global_device_ids=true | all-gather | bytes 393216 | tf_op jit(solution)/shard_map/all_gather | solution.py:28
  14.5 0.0 all-gather.6.cloned.1.call-update
  14.6 0.0 all-gather.8.cloned.1.call-start
  14.6 24.9 %all-gather.6.cloned.1.call-done = bf16[8,128,512]{2,1,0:T(8,128)(2,1)} async-done(((bf16[2,128,512]{2,1,0:T(8,128)(2,1)}), bf16[8,128,512]{2,1,0:T(8,128)(2,1)}) %all-gather.6.cloned.1.call-update) | async-done | bytes 1048592 | tf_op jit(solution)/shard_map/all_gather | solution.py:28
  39.5 0.0 all-gather.8.cloned.1.call-update
  39.5 0.0 all-gather.4.cloned.1.call-start
  39.6 0.7 compare_convert_fusion
  40.3 2.0 bitcast_multiply_fusion
  42.3 0.0 all-gather.4.cloned.1.call-update
  42.3 0.9 copy.20
  43.2 1.2 broadcast_in_dim.46
  44.4 8.6 %all-to-all-start = ((bf16[32,128,128]{1,2,0:T(8,128)(2,1)}), bf16[32,128,128]{1,2,0:T(8,128)(2,1)S(1)}, u32[]{:S(2)}, u32[]{:S(2)}) async-start(bf16[32,128,128]{1,2,0:T(8,128)(2,1)} %broadcast_in_dim.46), calls=%async_computation | async-start | bytes 2097152 | tf_op jit(solution)/shard_map/all_to_all | solution.py:41
  53.0 17.2 %copy.22 = bf16[1,2,32,16384]{2,1,3,0:T(2,128)(2,1)} copy(bf16[1,2,32,16384]{3,2,1,0:T(8,128)(2,1)} %param.14) | data formatting | bytes 4194304 | tf_op args[5]
  70.2 8.0 %bitcast_bitcast_fusion = bf16[16384,2,32]{2,1,0:T(2,128)(2,1)} fusion(bf16[1,2,32,16384]{2,1,3,0:T(2,128)(2,1)} %copy.22), kind=kLoop, calls=%fused_computation.22 | loop fusion | bytes 4194304
  78.2 18.2 %reshape.123 = bf16[32,2,16384]{2,1,0:T(2,128)(2,1)} reshape(bf16[16384,2,32]{2,1,0:T(2,128)(2,1)} %bitcast_bitcast_fusion) | data formatting | bytes 4194304
  96.4 0.0 all-to-all-done
  96.4 1.0 copy-done.2
  97.3 8.3 %all-to-all-start.2 = ((bf16[32,2,16384]{2,1,0:T(2,128)(2,1)}), bf16[32,2,16384]{2,1,0:T(2,128)(2,1)S(1)}, u32[]{:S(2)}, u32[]{:S(2)}) async-start(bf16[32,2,16384]{2,1,0:T(2,128)(2,1)} %reshape.123), calls=%async_computation.2 | async-start | bytes 4194304 | tf_op jit(solution)/shard_map/all_to_all | solution.py:76
  105.7 0.1 reshape.100
  105.7 0.1 broadcast_in_dim.41
  105.8 0.1 broadcast_in_dim.42
  105.9 1.7 convolution_convert_fusion
  107.6 41.9 %all-to-all-done.2 = bf16[32,2,16384]{2,1,0:T(2,128)(2,1)S(1)} async-done(((bf16[32,2,16384]{2,1,0:T(2,128)(2,1)}), bf16[32,2,16384]{2,1,0:T(2,128)(2,1)S(1)}, u32[]{:S(2)}, u32[]{:S(2)}) %all-to-all-start.2) | async-done | bytes 2097184 | tf_op jit(solution)/shard_map/all_to_all | solution.py:76
  149.6 1.2 broadcast_in_dim.47
  150.8 7.3 %all-to-all-start.1 = ((bf16[32,128,128]{2,1,0:T(8,128)(2,1)}), bf16[32,128,128]{2,1,0:T(8,128)(2,1)S(1)}, u32[]{:S(2)}, u32[]{:S(2)}) async-start(bf16[32,128,128]{2,1,0:T(8,128)(2,1)} %broadcast_in_dim.47), calls=%async_computation.1 | async-start | bytes 2097152 | tf_op jit(solution)/shard_map/all_to_all | solution.py:41
  158.1 6.6 %add_bitcast_fusion = f32[512,4096]{1,0:T(8,128)} fusion(bf16[1,512,4096]{2,1,0:T(8,128)(2,1)} %param.13), kind=kLoop, calls=%fused_computation.6 | loop fusion | flops 4194304 | bytes 12582912 | tf_op jit(solution)/shard_map/div | solution.py:73
  164.6 6.6 %reshape.124 = bf16[16384,2,32]{2,1,0:T(2,128)(2,1)} reshape(bf16[32,2,16384]{2,1,0:T(2,128)(2,1)S(1)} %all-to-all-done.2) | data formatting | bytes 4194304
  171.2 17.8 %copy.27 = bf16[2,32,32,512]{3,1,0,2:T(8,128)(2,1)} copy(bf16[2,32,32,512]{1,0,3,2:T(2,128)(2,1)} %bitcast.56) | data formatting | bytes 4194304 | tf_op jit(solution)/shard_map/all_to_all | solution.py:76
  189.0 129.3 %all-to-all-done.1 = bf16[32,128,128]{2,1,0:T(8,128)(2,1)S(1)} async-done(((bf16[32,128,128]{2,1,0:T(8,128)(2,1)}), bf16[32,128,128]{2,1,0:T(8,128)(2,1)S(1)}, u32[]{:S(2)}, u32[]{:S(2)}) %all-to-all-start.1) | async-done | bytes 1048608 | tf_op jit(solution)/shard_map/all_to_all | solution.py:41
  318.4 0.7 copy.21
  319.0 0.5 reshape_reshape.3
  319.5 2.2 gather_fusion.1
  321.7 0.2 bitcast_select_fusion.1
  321.9 0.0 all-gather.8.cloned.1.call-done
  321.9 4.6 %copy.18 = bf16[4,2,4,128,512]{4,3,2,1,0:T(8,128)(2,1)} copy(bf16[4,2,4,128,512]{4,3,1,0,2:T(8,128)(2,1)} %bitcast.60) | data formatting | bytes 8388608 | tf_op jit(solution)/shard_map/transpose | solution.py:32
  326.5 6.4 %copy.19 = bf16[128,32,512]{0,2,1:T(8,128)(2,1)} copy(bf16[128,32,512]{2,0,1:T(8,128)(2,1)} %bitcast.59) | data formatting | bytes 8388608 | tf_op jit(solution)/shard_map/transpose | solution.py:20
  332.9 9.4 %fusion.5 = bf16[128,512]{1,0:T(8,128)(2,1)S(1)} fusion(bf16[128,16384]{0,1:T(8,128)(2,1)} %bitcast.58, bf16[1,16384,512]{2,1,0:T(8,128)(2,1)} %param.11), kind=kOutput, calls=%fused_computation.10 | convolution fusion | flops 2147549184 | bytes 21102592 | tf_op jit(solution)/shard_map/dot_general | solution.py:61
  342.4 0.0 all-gather.4.cloned.1.call-done
  342.4 10.3 %gather_fusion = bf16[24,32,4096]{2,1,0:T(8,128)(2,1)} fusion(bf16[64,32,4096]{2,1,0:T(8,128)(2,1)} %all-gather.4.cloned.1.call-done, s32[1024]{0:T(1024)S(1)} %pad_clamp_fusion), kind=kCustom, calls=%fused_computation | custom fusion | bytes 12583008 | tf_op jit(solution)/shard_map/jit(_take)/gather | solution.py:81
  352.7 6.1 %bitcast_select_fusion = bf16[4,192,4096]{2,1,0:T(8,128)(2,1)} fusion(pred[4,192]{1,0:T(4,128)(4,1)S(1)} %broadcast_in_dim.42, bf16[4,192,4096]{2,1,0:T(8,128)(2,1)} %bitcast.57), kind=kLoop, calls=%fused_computation.7 | loop fusion | flops 3145728 | bytes 12583680 | tf_op jit(solution)/shard_map/jit(_take)/select_n | solution.py:81
  358.7 14.6 %fusion.4 = f32[4,192]{1,0:T(4,128)S(1)} fusion(bf16[4,192,512]{2,1,0:T(8,128)(2,1)S(1)} %bitcast_select_fusion.1, bf16[4,192,4096]{2,1,0:T(8,128)(2,1)} %bitcast_select_fusion, f32[512,4096]{1,0:T(8,128)} %add_bitcast_fusion, bf16[4,32,512]{2,1,0:T(8,128)(2,1)S(1)} %bitcast.65, bf16[4,32,4096]{2,1,0:T(8,128)(2,1)S(1)} %reshape_reshape.3), kind=kOutput, calls=%fused_computation.9 | convolution fusion | flops 3776052480 | bytes 16649216 | tf_op jit(solution)/shard_map/qfd,qkd->qkf/dot_general | solution.py:82
  373.3 6.4 %psum.35 = f32[4,192]{1,0:T(4,128)S(1)} all-reduce(f32[4,192]{1,0:T(4,128)S(1)} %fusion.4), channel_id=1, replica_groups=mesh['layer_0'=2,'layer_1'=2,'dp_0'=4,'dp_1'=2,'dp_2'=4] {'layer_0'}, use_global_device_ids=true, to_apply=%region_1.2 | all-reduce | flops 768 | bytes 6144 | tf_op jit(solution)/shard_map/psum | solution.py:51
  379.7 2.4 psum.36
  382.2 11.5 %psum.37 = f32[4,192]{1,0:T(4,128)S(1)} all-reduce(f32[4,192]{1,0:T(4,128)S(1)} %psum.36), channel_id=1, replica_groups=mesh['layer_0'=2,'layer_1'=2,'dp_0'=4,'dp_1'=2,'dp_2'=4] {'dp_0'}, use_global_device_ids=true, to_apply=%region_3.4 | all-reduce | flops 768 | bytes 6144 | tf_op jit(solution)/shard_map/psum | solution.py:51
  393.7 4.9 %psum.38 = f32[4,192]{1,0:T(4,128)S(1)} all-reduce(f32[4,192]{1,0:T(4,128)S(1)} %psum.37), channel_id=1, replica_groups=mesh['layer_0'=2,'layer_1'=2,'dp_0'=4,'dp_1'=2,'dp_2'=4] {'dp_1'}, use_global_device_ids=true, to_apply=%region_4.5 | all-reduce | flops 768 | bytes 6144 | tf_op jit(solution)/shard_map/psum | solution.py:51
  398.6 0.1 reshape.106
  398.7 14.3 %psum.39 = f32[4,6,32]{2,1,0:T(8,128)S(1)} all-reduce(f32[4,6,32]{2,1,0:T(8,128)S(1)} %reshape.106), channel_id=1, replica_groups=mesh['layer_0'=2,'layer_1'=2,'dp_0'=4,'dp_1'=2,'dp_2'=4] {'dp_2'}, use_global_device_ids=true, to_apply=%region_5.6 | all-reduce | flops 768 | bytes 6144 | tf_op jit(solution)/shard_map/psum | solution.py:51
  412.9 0.6 copy.25
  (12 shorter events, 0.0 us)
Async XLA Ops:
  6.5 99.4 %copy-start = (bf16[1,4096,128]{2,1,0:T(8,128)(2,1)S(1)}, bf16[1,4096,128]{2,1,0:T(8,128)(2,1)}, u32[]{:S(2)}) copy-start(bf16[1,4096,128]{2,1,0:T(8,128)(2,1)} %param.12) | copy-start | bytes 3145732
  6.5 33.0 %all-gather.6.cloned.1.call-start = ((), (), s32[]{:S(2)}) async-start(), calls=%async_computation.4 | async-start | bytes 1310720 | tf_op jit(solution)/shard_map/all_gather | solution.py:28
  14.6 307.4 %all-gather.8.cloned.1.call-start = ((), (), s32[]{:S(2)}) async-start(), calls=%async_computation.5 | async-start | bytes 5242880 | tf_op jit(solution)/shard_map/all_gather | solution.py:28
  39.5 302.9 %all-gather.4.cloned.1.call-start = ((), (), s32[]{:S(2)}) async-start(), calls=%async_computation.3 | async-start | bytes 17301504 | tf_op jit(solution)/shard_map/all_gather | solution.py:80
  44.4 52.0 %all-to-all-start = ((bf16[32,128,128]{1,2,0:T(8,128)(2,1)}), bf16[32,128,128]{1,2,0:T(8,128)(2,1)S(1)}, u32[]{:S(2)}, u32[]{:S(2)}) async-start(bf16[32,128,128]{1,2,0:T(8,128)(2,1)} %broadcast_in_dim.46), calls=%async_computation | async-start | bytes 2097152 | tf_op jit(solution)/shard_map/all_to_all | solution.py:41
  78.2 27.4 %copy-start.3 = (s32[4,6]{1,0:T(4,128)S(1)}, s32[4,6]{1,0:T(4,128)}, u32[]{:S(2)}) copy-start(s32[4,6]{1,0:T(4,128)} %param.17) | copy-start | bytes 292
  96.4 1.0 copy-start.2
  97.3 52.2 %all-to-all-start.2 = ((bf16[32,2,16384]{2,1,0:T(2,128)(2,1)}), bf16[32,2,16384]{2,1,0:T(2,128)(2,1)S(1)}, u32[]{:S(2)}, u32[]{:S(2)}) async-start(bf16[32,2,16384]{2,1,0:T(2,128)(2,1)} %reshape.123), calls=%async_computation.2 | async-start | bytes 4194304 | tf_op jit(solution)/shard_map/all_to_all | solution.py:76
  150.8 167.6 %all-to-all-start.1 = ((bf16[32,128,128]{2,1,0:T(8,128)(2,1)}), bf16[32,128,128]{2,1,0:T(8,128)(2,1)S(1)}, u32[]{:S(2)}, u32[]{:S(2)}) async-start(bf16[32,128,128]{2,1,0:T(8,128)(2,1)} %broadcast_in_dim.47), calls=%async_computation.1 | async-start | bytes 2097152 | tf_op jit(solution)/shard_map/all_to_all | solution.py:41
  358.7 54.8 %copy-start.1 = (bf16[1,4096,128]{2,1,0:T(8,128)(2,1)S(1)}, bf16[1,4096,128]{2,1,0:T(8,128)(2,1)}, u32[]{:S(2)}) copy-start(bf16[1,4096,128]{2,1,0:T(8,128)(2,1)} %param.12) | copy-start | bytes 3145732
Sparse Core Ops, SparseCore 0:
  14.7 24.7 all-gather.5
  41.2 58.4 all-gather.7
  101.3 218.5 all-gather.3
where the time goes:
time: 422 us; the launch traced here: 420 us
  waiting for transfers between devices  196 us (46%)
  local copies, waits for them, and re-layouts  97.6 us (23%)
  blocking collectives  47.6 us (11%)
  matrix products  25.7 us (6%)
  starting transfers between devices  24.3 us (6%)
  other arithmetic  15.5 us (4%)
  between operations  13.2 us (3%)
    all_to_all x2, waiting for transfers between devices, from_everyone(): lax.all_to_all(jnp.broadcast_to(value[None], (count, *value.shape)), axis...  129 us
    unnamed x12, local copies, waits for them, and re-layouts  50.9 us
    all_to_all x1, waiting for transfers between devices, on_device(): lax.all_to_all(out_store[0], DP, split_axis=2, concat_axis=0, tiled=True)  41.9 us
    psum x5, blocking collectives, over_axes(): return functools.reduce(lax.psum, axes, value)  39.6 us
    all_gather x2, waiting for transfers between devices, all_blocks(): blocks = lax.all_gather(blocks, axes[k], axis=0, tiled=True)  24.9 us
    all_to_all x1, local copies, waits for them, and re-layouts, on_device(): lax.all_to_all(out_store[0], DP, split_axis=2, concat_axis=0, tiled=True)  17.8 us
    all_to_all x2, starting transfers between devices, from_everyone(): lax.all_to_all(jnp.broadcast_to(value[None], (count, *value.shape)), axis...  15.9 us
    dot_general x1, matrix products, on_device(): jnp.einsum('qfd,qkd->qkf', precond, right_rows, preferred_element_type=jn...  14.6 us
  transfers between devices with their start and end apart: 6, of which 3 were waited for; matrix products, arithmetic and copies ran while one was open for 25% of the time, Pallas kernels for 0%

commit v1 on v0

--- a/solution.py
+++ b/solution.py
@@ -25,7 +25,9 @@
 def all_blocks(value, axes, turns):
     blocks = value[None]
     for k in turns:
-        blocks = lax.all_gather(blocks, axes[k], axis=0, tiled=True)
+        blocks = jnp.concatenate(
+            lax.all_to_all(jnp.stack([blocks] * lax.axis_size(axes[k])), axes[k], 0, 0), axis=0
+        )
     block = [lax.axis_size(axes[k]) for k in reversed(turns)]
     blocks = blocks.reshape(*block, *value.shape)
     turned = sorted(range(len(turns)), key=lambda place: turns[len(turns) - 1 - place])

time: 422 us -> 456 us (1.081)
  starting transfers between devices: 24.3 us -> 191 us
  waiting for transfers between devices: 196 us -> 36.1 us
  blocking collectives: 47.6 us -> 68.6 us
    all_to_all x2 -> x1, starting transfers between devices: 15.9 us -> 173 us  [from_everyone(): lax.all_to_all(jnp.broadcast_to(value[None], (count, *value.shape)), axis...]
    all_to_all x2 -> x1, waiting for transfers between devices: 129 us -> 0.01 us  [from_everyone(): lax.all_to_all(jnp.broadcast_to(value[None], (count, *value.shape)), axis...]
    all_to_all x0 -> x2, blocking collectives: none -> 30.3 us  [the longest x1 22.1 us: from_everyone(): lax.all_to_all(jnp.broadcast_to(value[None], (count, *value.shape)), axis...]
    all_gather x2 -> x0, waiting for transfers between devices: 24.9 us -> none  [all_blocks(): blocks = lax.all_gather(blocks, axes[k], axis=0, tiled=True)]
    all_to_all x1, waiting for transfers between devices: 41.9 us -> 24.8 us  [on_device(): lax.all_to_all(out_store[0], DP, split_axis=2, concat_axis=0, tiled=True)]
    all_to_all x0 -> x2, waiting for transfers between devices: none -> 11.3 us  [all_blocks(): lax.all_to_all(jnp.stack([blocks] * lax.axis_size(axes[k])), axes[k], 0, 0)]
    all_to_all x0 -> x2, starting transfers between devices: none -> 10.1 us  [all_blocks(): lax.all_to_all(jnp.stack([blocks] * lax.axis_size(axes[k])), axes[k], 0, 0)]
    all_gather x1 -> x0, blocking collectives: 8 us -> none  [all_blocks(): blocks = lax.all_gather(blocks, axes[k], axis=0, tiled=True)]
  transfers between devices with their start and end apart: 6 -> 5, of which waited for: 3 -> 2; matrix products, arithmetic and copies ran while one was open for 25% -> 24% of each run, Pallas kernels for 0% -> 0%
where the time goes in v1:
time: 456 us; the launch traced here: 452 us
  starting transfers between devices  191 us (42%)
  local copies, waits for them, and re-layouts  101 us (22%)
  blocking collectives  68.6 us (15%)
  waiting for transfers between devices  36.1 us (8%)
  matrix products  25.7 us (6%)
  other arithmetic  16.6 us (4%)
  between operations  13.5 us (3%)
    all_to_all x1, starting transfers between devices, from_everyone(): lax.all_to_all(jnp.broadcast_to(value[None], (count, *value.shape)), axis...  173 us
    unnamed x16, local copies, waits for them, and re-layouts  50.9 us
    psum x5, blocking collectives, over_axes(): return functools.reduce(lax.psum, axes, value)  38.3 us
    all_to_all x1, waiting for transfers between devices, on_device(): lax.all_to_all(out_store[0], DP, split_axis=2, concat_axis=0, tiled=True)  24.8 us
    all_to_all x1, blocking collectives, from_everyone(): lax.all_to_all(jnp.broadcast_to(value[None], (count, *value.shape)), axis...  22.1 us
    all_to_all x1, local copies, waits for them, and re-layouts, on_device(): lax.all_to_all(out_store[0], DP, split_axis=2, concat_axis=0, tiled=True)  17.8 us
    dot_general x1, matrix products, on_device(): jnp.einsum('qfd,qkd->qkf', precond, right_rows, preferred_element_type=jn...  14.6 us
    all_to_all x2, waiting for transfers between devices, all_blocks(): lax.all_to_all(jnp.stack([blocks] * lax.axis_size(axes[k])), axes[k], 0, 0)  11.3 us
  transfers between devices with their start and end apart: 5, of which 2 were waited for; matrix products, arithmetic and copies ran while one was open for 24% of the time, Pallas kernels for 0%

profile of v1, /device:TPU:8, one launch (start us, length us, event | category | flops | bytes accessed | tf_op | source)
XLA Modules:
  0.0 452.5 jit_solution(9781915603679080227)
XLA Ops:
  6.5 0.8 compare_convert_fusion
  7.4 1.9 bitcast_multiply_fusion
  9.3 0.0 all-gather.2.cloned.1.call-update
  9.3 1.0 pad_maximum_fusion
  10.3 8.2 %all_to_all.43 = bf16[2,1,128,512]{3,2,1,0:T(8,128)(2,1)S(1)} all-to-all(bf16[2,1,128,512]{3,2,1,0:T(8,128)(2,1)S(1)} %pad_maximum_fusion), channel_id=1, replica_groups=mesh['layer_0'=2,'layer_1'=2,'dp_0'=4,'dp_1'=2,'dp_2'=4] {'dp_1'}, dimensions={0} | all-to-all | bytes 524288 | tf_op jit(solution)/shard_map/all_to_all | solution.py:29
  18.5 1.2 stack.10
  19.7 5.0 %all-to-all-start.1 = ((bf16[4,2,128,512]{3,2,1,0:T(8,128)(2,1)}), bf16[4,2,128,512]{3,2,1,0:T(8,128)(2,1)S(1)}, u32[]{:S(2)}, u32[]{:S(2)}) async-start(bf16[4,2,128,512]{3,2,1,0:T(8,128)(2,1)} %stack.10), calls=%async_computation.1 | async-start | bytes 2097152 | tf_op jit(solution)/shard_map/all_to_all | solution.py:29
  24.7 17.2 %copy.21 = bf16[1,2,32,16384]{2,1,3,0:T(2,128)(2,1)} copy(bf16[1,2,32,16384]{3,2,1,0:T(8,128)(2,1)} %param.14) | data formatting | bytes 4194304 | tf_op args[5]
  41.9 0.1 copy.19
  42.0 0.0 all-to-all-done.1
  42.0 1.3 broadcast_in_dim.46
  43.3 172.8 %all-to-all-start.3 = ((bf16[32,128,128]{1,2,0:T(8,128)(2,1)}), bf16[32,128,128]{1,2,0:T(8,128)(2,1)S(1)}, u32[]{:S(2)}, u32[]{:S(2)}) async-start(bf16[32,128,128]{1,2,0:T(8,128)(2,1)} %broadcast_in_dim.46), calls=%async_computation.3 | async-start | bytes 2097152 | tf_op jit(solution)/shard_map/all_to_all | solution.py:43
  216.1 8.0 %bitcast_bitcast_fusion = bf16[16384,2,32]{2,1,0:T(2,128)(2,1)} fusion(bf16[1,2,32,16384]{2,1,3,0:T(2,128)(2,1)} %copy.21), kind=kLoop, calls=%fused_computation.23 | loop fusion | bytes 4194304
  224.1 18.2 %reshape.123 = bf16[32,2,16384]{2,1,0:T(2,128)(2,1)} reshape(bf16[16384,2,32]{2,1,0:T(2,128)(2,1)} %bitcast_bitcast_fusion) | data formatting | bytes 4194304
  242.2 0.0 all-to-all-done.3
  242.2 1.0 copy-done.3
  243.2 8.3 %all-to-all-start.5 = ((bf16[32,2,16384]{2,1,0:T(2,128)(2,1)}), bf16[32,2,16384]{2,1,0:T(2,128)(2,1)S(1)}, u32[]{:S(2)}, u32[]{:S(2)}) async-start(bf16[32,2,16384]{2,1,0:T(2,128)(2,1)} %reshape.123), calls=%async_computation.5 | async-start | bytes 4194304 | tf_op jit(solution)/shard_map/all_to_all | solution.py:78
  251.5 1.7 convolution_convert_fusion
  253.2 24.8 %all-to-all-done.5 = bf16[32,2,16384]{2,1,0:T(2,128)(2,1)S(1)} async-done(((bf16[32,2,16384]{2,1,0:T(2,128)(2,1)}), bf16[32,2,16384]{2,1,0:T(2,128)(2,1)S(1)}, u32[]{:S(2)}, u32[]{:S(2)}) %all-to-all-start.5) | async-done | bytes 2097184 | tf_op jit(solution)/shard_map/all_to_all | solution.py:78
  278.1 0.2 broadcast_in_dim.47
  278.3 22.1 %all_to_all.44 = bf16[32,128,128]{2,1,0:T(8,128)(2,1)S(1)} all-to-all(bf16[32,128,128]{2,1,0:T(8,128)(2,1)S(1)} %broadcast_in_dim.47), channel_id=1, replica_groups=mesh['layer_0'=2,'layer_1'=2,'dp_0'=4,'dp_1'=2,'dp_2'=4] {'dp_0','dp_1',..., dimensions={0} | all-to-all | bytes 2097152 | tf_op jit(solution)/shard_map/all_to_all | solution.py:43
  300.4 3.7 stack.11
  304.1 5.0 %all-to-all-start.2 = ((bf16[4,8,128,512]{3,2,1,0:T(8,128)(2,1)}), bf16[4,8,128,512]{3,2,1,0:T(8,128)(2,1)}, u32[]{:S(2)}, u32[]{:S(2)}) async-start(bf16[4,8,128,512]{3,2,1,0:T(8,128)(2,1)} %stack.11), calls=%async_computation.2 | async-start | bytes 8388608 | tf_op jit(solution)/shard_map/all_to_all | solution.py:29
  309.1 0.1 reshape.101
  309.2 0.1 broadcast_in_dim.41
  309.3 0.1 broadcast_in_dim.42
  309.4 6.6 %add_bitcast_fusion = f32[512,4096]{1,0:T(8,128)} fusion(bf16[1,512,4096]{2,1,0:T(8,128)(2,1)} %param.13), kind=kLoop, calls=%fused_computation.6 | loop fusion | flops 4194304 | bytes 12582912 | tf_op jit(solution)/shard_map/div | solution.py:75
  316.0 6.6 %reshape.124 = bf16[16384,2,32]{2,1,0:T(2,128)(2,1)} reshape(bf16[32,2,16384]{2,1,0:T(2,128)(2,1)S(1)} %all-to-all-done.5) | data formatting | bytes 4194304
  322.6 17.8 %copy.26 = bf16[2,32,32,512]{3,1,0,2:T(8,128)(2,1)} copy(bf16[2,32,32,512]{1,0,3,2:T(2,128)(2,1)} %bitcast.60) | data formatting | bytes 4194304 | tf_op jit(solution)/shard_map/all_to_all | solution.py:78
  340.4 0.7 copy.20
  341.1 0.5 reshape_reshape.7
  341.6 2.2 gather_fusion.1
  343.8 0.2 bitcast_select_fusion.1
  343.9 11.3 %all-to-all-done.2 = bf16[4,8,128,512]{3,2,1,0:T(8,128)(2,1)} async-done(((bf16[4,8,128,512]{3,2,1,0:T(8,128)(2,1)}), bf16[4,8,128,512]{3,2,1,0:T(8,128)(2,1)}, u32[]{:S(2)}, u32[]{:S(2)}) %all-to-all-start.2) | async-done | bytes 4194336 | tf_op jit(solution)/shard_map/all_to_all | solution.py:29
  355.2 4.6 %copy.17 = bf16[4,8,128,512]{3,2,0,1:T(8,128)(2,1)} copy(bf16[4,8,128,512]{3,2,1,0:T(8,128)(2,1)} %all-to-all-done.2) | data formatting | bytes 8388608 | tf_op jit(solution)/shard_map/all_to_all | solution.py:29
  359.8 6.4 %copy.18 = bf16[128,32,512]{0,2,1:T(8,128)(2,1)} copy(bf16[128,32,512]{2,0,1:T(8,128)(2,1)} %bitcast.63) | data formatting | bytes 8388608 | tf_op jit(solution)/shard_map/transpose | solution.py:20
  366.2 9.4 %fusion.5 = bf16[128,512]{1,0:T(8,128)(2,1)S(1)} fusion(bf16[128,16384]{0,1:T(8,128)(2,1)} %bitcast.62, bf16[1,16384,512]{2,1,0:T(8,128)(2,1)} %param.11), kind=kOutput, calls=%fused_computation.10 | convolution fusion | flops 2147549184 | bytes 21102592 | tf_op jit(solution)/shard_map/dot_general | solution.py:63
  375.7 0.0 all-gather.2.cloned.1.call-done
  375.7 10.3 %gather_fusion = bf16[24,32,4096]{2,1,0:T(8,128)(2,1)} fusion(bf16[64,32,4096]{2,1,0:T(8,128)(2,1)} %all-gather.2.cloned.1.call-done, s32[1024]{0:T(1024)S(1)} %pad_clamp_fusion), kind=kCustom, calls=%fused_computation | custom fusion | bytes 12583008 | tf_op jit(solution)/shard_map/jit(_take)/gather | solution.py:83
  386.0 6.1 %bitcast_select_fusion = bf16[4,192,4096]{2,1,0:T(8,128)(2,1)} fusion(pred[4,192]{1,0:T(4,128)(4,1)S(1)} %broadcast_in_dim.42, bf16[4,192,4096]{2,1,0:T(8,128)(2,1)} %bitcast.61), kind=kLoop, calls=%fused_computation.7 | loop fusion | flops 3145728 | bytes 12583680 | tf_op jit(solution)/shard_map/jit(_take)/select_n | solution.py:83
  392.0 14.6 %fusion.4 = f32[4,192]{1,0:T(4,128)S(1)} fusion(bf16[4,192,512]{2,1,0:T(8,128)(2,1)S(1)} %bitcast_select_fusion.1, bf16[4,192,4096]{2,1,0:T(8,128)(2,1)} %bitcast_select_fusion, f32[512,4096]{1,0:T(8,128)} %add_bitcast_fusion, bf16[4,32,512]{2,1,0:T(8,128)(2,1)S(1)} %bitcast.70, bf16[4,32,4096]{2,1,0:T(8,128)(2,1)S(1)} %reshape_reshape.7), kind=kOutput, calls=%fused_computation.9 | convolution fusion | flops 3776052480 | bytes 16649216 | tf_op jit(solution)/shard_map/qfd,qkd->qkf/dot_general | solution.py:84
  406.6 6.4 %psum.35 = f32[4,192]{1,0:T(4,128)S(1)} all-reduce(f32[4,192]{1,0:T(4,128)S(1)} %fusion.4), channel_id=1, replica_groups=mesh['layer_0'=2,'layer_1'=2,'dp_0'=4,'dp_1'=2,'dp_2'=4] {'layer_0'}, use_global_device_ids=true, to_apply=%region_1.2 | all-reduce | flops 768 | bytes 6144 | tf_op jit(solution)/shard_map/psum | solution.py:53
  413.1 2.4 psum.36
  415.5 9.2 %psum.37 = f32[4,192]{1,0:T(4,128)S(1)} all-reduce(f32[4,192]{1,0:T(4,128)S(1)} %psum.36), channel_id=1, replica_groups=mesh['layer_0'=2,'layer_1'=2,'dp_0'=4,'dp_1'=2,'dp_2'=4] {'dp_0'}, use_global_device_ids=true, to_apply=%region_3.4 | all-reduce | flops 768 | bytes 6144 | tf_op jit(solution)/shard_map/psum | solution.py:53
  424.7 4.9 %psum.38 = f32[4,192]{1,0:T(4,128)S(1)} all-reduce(f32[4,192]{1,0:T(4,128)S(1)} %psum.37), channel_id=1, replica_groups=mesh['layer_0'=2,'layer_1'=2,'dp_0'=4,'dp_1'=2,'dp_2'=4] {'dp_1'}, use_global_device_ids=true, to_apply=%region_4.5 | all-reduce | flops 768 | bytes 6144 | tf_op jit(solution)/shard_map/psum | solution.py:53
  429.6 0.1 reshape.106
  429.7 15.3 %psum.39 = f32[4,6,32]{2,1,0:T(8,128)S(1)} all-reduce(f32[4,6,32]{2,1,0:T(8,128)S(1)} %reshape.106), channel_id=1, replica_groups=mesh['layer_0'=2,'layer_1'=2,'dp_0'=4,'dp_1'=2,'dp_2'=4] {'dp_2'}, use_global_device_ids=true, to_apply=%region_5.6 | all-reduce | flops 768 | bytes 6144 | tf_op jit(solution)/shard_map/psum | solution.py:53
  445.0 0.6 copy.24
  (16 shorter events, 0.0 us)
Async XLA Ops:
  6.5 245.0 %copy-start = (bf16[1,4096,128]{2,1,0:T(8,128)(2,1)S(1)}, bf16[1,4096,128]{2,1,0:T(8,128)(2,1)}, u32[]{:S(2)}) copy-start(bf16[1,4096,128]{2,1,0:T(8,128)(2,1)} %param.12) | copy-start | bytes 3145732
  6.5 369.1 %all-gather.2.cloned.1.call-start = ((), (), s32[]{:S(2)}) async-start(), calls=%async_computation.6 | async-start | bytes 17301504 | tf_op jit(solution)/shard_map/all_gather | solution.py:82
  19.7 22.2 %copy-start.4 = (bf16[1,128,128]{2,1,0:T(8,128)(2,1)S(1)}, bf16[1,128,128]{2,1,0:T(8,128)(2,1)}, u32[]{:S(2)}) copy-start(bf16[1,128,128]{2,1,0:T(8,128)(2,1)} %param.10) | copy-start | bytes 98308
  19.7 22.3 %all-to-all-start.1 = ((bf16[4,2,128,512]{3,2,1,0:T(8,128)(2,1)}), bf16[4,2,128,512]{3,2,1,0:T(8,128)(2,1)S(1)}, u32[]{:S(2)}, u32[]{:S(2)}) async-start(bf16[4,2,128,512]{3,2,1,0:T(8,128)(2,1)} %stack.10), calls=%async_computation.1 | async-start | bytes 2097152 | tf_op jit(solution)/shard_map/all_to_all | solution.py:29
  42.0 182.1 %copy-start.2 = (bf16[4,2,128,512]{3,2,1,0:T(8,128)(2,1)}, bf16[4,2,128,512]{3,2,1,0:T(8,128)(2,1)S(1)}, u32[]{:S(2)}) copy-start(bf16[4,2,128,512]{3,2,1,0:T(8,128)(2,1)S(1)} %all-to-all-done.1) | copy-start | bytes 3145732
  43.3 198.9 %all-to-all-start.3 = ((bf16[32,128,128]{1,2,0:T(8,128)(2,1)}), bf16[32,128,128]{1,2,0:T(8,128)(2,1)S(1)}, u32[]{:S(2)}, u32[]{:S(2)}) async-start(bf16[32,128,128]{1,2,0:T(8,128)(2,1)} %broadcast_in_dim.46), calls=%async_computation.3 | async-start | bytes 2097152 | tf_op jit(solution)/shard_map/all_to_all | solution.py:43
  242.2 1.0 copy-start.3
  243.2 34.8 %all-to-all-start.5 = ((bf16[32,2,16384]{2,1,0:T(2,128)(2,1)}), bf16[32,2,16384]{2,1,0:T(2,128)(2,1)S(1)}, u32[]{:S(2)}, u32[]{:S(2)}) async-start(bf16[32,2,16384]{2,1,0:T(2,128)(2,1)} %reshape.123), calls=%async_computation.5 | async-start | bytes 4194304 | tf_op jit(solution)/shard_map/all_to_all | solution.py:78
  300.4 8.7 %copy-start.5 = (s32[4,6]{1,0:T(4,128)S(1)}, s32[4,6]{1,0:T(4,128)}, u32[]{:S(2)}) copy-start(s32[4,6]{1,0:T(4,128)} %param.17) | copy-start | bytes 292
  304.1 51.2 %all-to-all-start.2 = ((bf16[4,8,128,512]{3,2,1,0:T(8,128)(2,1)}), bf16[4,8,128,512]{3,2,1,0:T(8,128)(2,1)}, u32[]{:S(2)}, u32[]{:S(2)}) async-start(bf16[4,8,128,512]{3,2,1,0:T(8,128)(2,1)} %stack.11), calls=%async_computation.2 | async-start | bytes 8388608 | tf_op jit(solution)/shard_map/all_to_all | solution.py:29
  392.0 53.6 %copy-start.1 = (bf16[1,4096,128]{2,1,0:T(8,128)(2,1)S(1)}, bf16[1,4096,128]{2,1,0:T(8,128)(2,1)}, u32[]{:S(2)}) copy-start(bf16[1,4096,128]{2,1,0:T(8,128)(2,1)} %param.12) | copy-start | bytes 3145732
Sparse Core Ops, SparseCore 0:
  9.4 190.7 all-gather.1
